TPU v7x, 32 devices: a whole 2x2x4 slice. The times are simulated.
32 devices in a mesh: ep: 4 (over x, core), fsdp: 8 (over z, y).
Axes of the slice: x: 2, y: 2, z: 4, core: 2. Of those that a mesh axis runs over, the one named last changes fastest.
Arguments:
- master_gate: float32 [128, 2048, 768], P('ep', 'fsdp'), may hold values from -0.1875 to 0.1875
- master_up: float32 [128, 2048, 768], P('ep', 'fsdp'), may hold values from -0.1875 to 0.1875
- router_weight: float32 [2048, 128], P('fsdp', 'ep'), may hold values from -0.125 to 0.125
- router_gain: float32 [2048], P('fsdp'), may hold values from 0.25 to 1.75
Outputs:
- final_gate: bfloat16 [128, 2048, 768], P(('ep', 'fsdp'))
- final_up: bfloat16 [128, 2048, 768], P(('ep', 'fsdp'))
- scale_gate: float32 [128, 768], P(('ep', 'fsdp'))
- scale_up: float32 [128, 768], P(('ep', 'fsdp'))
- serve_router: bfloat16 [2048, 128], replicated
All inputs are finite; a program needn't handle non-finite values.
Results may differ from a plain program's by a relative error of at most 0.001.
Values may be sent and summed in bfloat16 or wider, within the bound.
A program may use at most 192 MiB of HBM per device.

v0:
```python
import jax
import jax.numpy as jnp
from jax import lax
from jax.sharding import PartitionSpec as P


def body(master_gate, master_up, router_weight, router_gain):
    total_gate, total_up = lax.psum(
        (jnp.sum(master_gate * master_gate, axis=1), jnp.sum(master_up * master_up, axis=1)), "fsdp"
    )
    scale_gate = jnp.sqrt(total_gate)
    scale_up = jnp.sqrt(total_up)
    narrow_gate, narrow_up = (
        (master_gate / jnp.expand_dims(scale_gate, 1)).astype(jnp.bfloat16),
        (master_up / jnp.expand_dims(scale_up, 1)).astype(jnp.bfloat16),
    )
    final_gate, final_up = (
        lax.all_to_all(narrow_gate, "fsdp", split_axis=0, concat_axis=1, tiled=True),
        lax.all_to_all(narrow_up, "fsdp", split_axis=0, concat_axis=1, tiled=True),
    )
    scale_gate = lax.dynamic_slice_in_dim(
        scale_gate, lax.axis_index("fsdp") * final_gate.shape[0], final_gate.shape[0], axis=0
    )
    scale_up = lax.dynamic_slice_in_dim(
        scale_up, lax.axis_index("fsdp") * final_up.shape[0], final_up.shape[0], axis=0
    )
    part_router = (router_weight * router_gain[:, None]).astype(jnp.bfloat16)
    row_router = lax.all_gather(part_router, "fsdp", axis=0, tiled=True)
    serve_router = lax.all_gather(row_router, "ep", axis=1, tiled=True)
    return (final_gate, final_up, scale_gate, scale_up, serve_router)


def solution(mesh):
    return jax.shard_map(
        body,
        mesh=mesh,
        in_specs=(P("ep", "fsdp", None), P("ep", "fsdp", None), P("fsdp", "ep"), P("fsdp")),
        out_specs=(
            P(("ep", "fsdp"), None, None),
            P(("ep", "fsdp"), None, None),
            P(("ep", "fsdp"), None),
            P(("ep", "fsdp"), None),
            P(),
        ),
        check_vma=False,
    )
```

profile of v0, /device:TPU:12, one launch (start us, length us, event | category | flops | bytes accessed | tf_op | source)
XLA Modules:
  0.0 719.5 jit_solution(15116092223100259474)
XLA Ops:
  7.2 0.0 all-reduce.3.cloned.1.call-start
  7.2 17.3 %multiply_reduce_fusion = (f32[32,768]{1,0:T(8,128)}, f32[32,768]{1,0:T(8,128)}) fusion(f32[32,256,768]{2,1,0:T(8,128)} %param.5, f32[32,256,768]{2,1,0:T(8,128)} %param.4), kind=kLoop, calls=%fused_computation.1 | loop fusion | flops 25116672 | bytes 50528256 | tf_op jit(solution)/shard_map/reduce_sum | solution.py:9
  24.5 0.0 all-reduce.3.cloned.1.call-update
  24.5 71.4 %all-reduce.3.cloned.1.call-done = (f32[32,768]{1,0:T(8,128)}, f32[32,768]{1,0:T(8,128)}) async-done(((f32[32,768]{1,0:T(8,128)}, f32[32,768]{1,0:T(8,128)}), (f32[32,768]{1,0:T(8,128)}, f32[32,768]{1,0:T(8,128)})) %all-reduce.3.cloned.1.call-update) | async-done | bytes 196624 | tf_op jit(solution)/shard_map/psum | solution.py:8
  95.9 0.9 sqrt.6
  96.8 0.0 copy-start
  96.8 13.7 %divide_convert_fusion.1 = bf16[32,256,768]{2,1,0:T(8,128)(2,1)} fusion(f32[32,256,768]{2,1,0:T(8,128)} %param.4, f32[32,768]{1,0:T(8,128)S(1)} %sqrt.6), kind=kLoop, calls=%fused_computation.2 | loop fusion | flops 12582912 | bytes 37847040 | tf_op jit(solution)/shard_map/convert_element_type | solution.py:14
  110.5 6.6 all-to-all-start
  117.0 0.0 copy-done
  117.0 0.0 copy-start.1
  117.1 0.0 copy-start.2
  117.1 13.8 %divide_convert_fusion = bf16[32,256,768]{2,1,0:T(8,128)(2,1)} fusion(f32[32,256,768]{2,1,0:T(8,128)} %param.5, f32[32,768]{1,0:T(8,128)S(1)} %sqrt.7), kind=kLoop, calls=%fused_computation | loop fusion | flops 12582912 | bytes 37847040 | tf_op jit(solution)/shard_map/convert_element_type | solution.py:15
  130.9 254.0 %all-to-all-done = bf16[32,256,768]{2,1,0:T(8,128)(2,1)} async-done(((bf16[32,256,768]{2,1,0:T(8,128)(2,1)}), bf16[32,256,768]{2,1,0:T(8,128)(2,1)}, u32[]{:S(2)}, u32[]{:S(2)}) %all-to-all-start) | async-done | bytes 12582944 | tf_op jit(solution)/shard_map/all_to_all | solution.py:18
  384.9 8.7 %all-to-all-start.1 = ((bf16[32,256,768]{2,1,0:T(8,128)(2,1)}), bf16[32,256,768]{2,1,0:T(8,128)(2,1)}, u32[]{:S(2)}, u32[]{:S(2)}) async-start(bf16[32,256,768]{2,1,0:T(8,128)(2,1)} %divide_convert_fusion), calls=%async_computation.1 | async-start | bytes 25165824 | tf_op jit(solution)/shard_map/all_to_all | solution.py:19
  393.6 0.0 copy-done.1
  393.6 0.0 copy-done.2
  393.6 288.4 %all_gather.6 = bf16[2048,32]{0,1:T(8,128)(2,1)S(1)} all-gather(bf16[256,32]{0,1:T(8,128)(2,1)S(1)} %multiply_convert_fusion), channel_id=1, replica_groups=mesh['ep'=4,'fsdp'=8] {'fsdp'}, dimensions={0}, use_global_device_ids=true | all-gather | bytes 147456 | tf_op jit(solution)/shard_map/all_gather | solution.py:28
  682.0 7.1 all_gather.7
  689.1 1.0 copy.14
  690.1 0.6 constant_dynamic-slice_fusion
  690.7 0.6 constant_dynamic-slice_fusion.1
  691.3 10.7 %copy.12 = bf16[8,4,256,768]{3,2,0,1:T(8,128)(2,1)} copy(bf16[8,4,256,768]{3,2,1,0:T(8,128)(2,1)} %bitcast) | data formatting | bytes 25165824 | tf_op jit(solution)/shard_map/all_to_all | solution.py:18
  702.0 0.0 all-to-all-done.1
  702.0 10.7 %copy.13 = bf16[8,4,256,768]{3,2,0,1:T(8,128)(2,1)} copy(bf16[8,4,256,768]{3,2,1,0:T(8,128)(2,1)} %bitcast.3) | data formatting | bytes 25165824 | tf_op jit(solution)/shard_map/all_to_all | solution.py:19
  (2 shorter events, 0.0 us)
Async XLA Ops:
  7.2 88.7 %all-reduce.3.cloned.1.call-start = ((), (), s32[]{:S(2)}) async-start(), calls=%async_computation.2 | async-start | bytes 393216 | tf_op jit(solution)/shard_map/psum | solution.py:8
  96.8 20.2 %copy-start = (f32[32,768]{1,0:T(8,128)S(1)}, f32[32,768]{1,0:T(8,128)}, u32[]{:S(2)}) copy-start(f32[32,768]{1,0:T(8,128)} %get-tuple-element.11) | copy-start | bytes 294916
  110.5 274.4 %all-to-all-start = ((bf16[32,256,768]{2,1,0:T(8,128)(2,1)}), bf16[32,256,768]{2,1,0:T(8,128)(2,1)}, u32[]{:S(2)}, u32[]{:S(2)}) async-start(bf16[32,256,768]{2,1,0:T(8,128)(2,1)} %divide_convert_fusion.1), calls=%async_computation | async-start | bytes 25165824 | tf_op jit(solution)/shard_map/all_to_all | solution.py:18
  117.0 276.5 %copy-start.1 = (f32[256,32]{0,1:T(8,128)S(1)}, f32[256,32]{0,1:T(8,128)}, u32[]{:S(2)}) copy-start(f32[256,32]{0,1:T(8,128)} %param.6) | copy-start | bytes 98308
  117.1 276.5 %copy-start.2 = (f32[256]{0:T(256)S(1)}, f32[256]{0:T(256)}, u32[]{:S(2)}) copy-start(f32[256]{0:T(256)} %param.7) | copy-start | bytes 3076
  384.9 317.1 %all-to-all-start.1 = ((bf16[32,256,768]{2,1,0:T(8,128)(2,1)}), bf16[32,256,768]{2,1,0:T(8,128)(2,1)}, u32[]{:S(2)}, u32[]{:S(2)}) async-start(bf16[32,256,768]{2,1,0:T(8,128)(2,1)} %divide_convert_fusion), calls=%async_computation.1 | async-start | bytes 25165824 | tf_op jit(solution)/shard_map/all_to_all | solution.py:19
Sparse Core Ops, SparseCore 0:
  24.6 71.1 all-reduce.2
where the time goes:
time: 724 us; the launch traced here: 720 us
  waiting for transfers between devices  325 us (45%)
  blocking collectives  296 us (41%)
  other arithmetic  44.7 us (6%)
  local copies, waits for them, and re-layouts  24.5 us (3%)
  starting transfers between devices  15.3 us (2%)
  between operations  14.1 us (2%)
    all_gather x1, blocking collectives, body(): row_router = lax.all_gather(part_router, 'fsdp', axis=0, tiled=True)  288 us
    all_to_all x1, waiting for transfers between devices, body(): lax.all_to_all(narrow_gate, 'fsdp', split_axis=0, concat_axis=1, tiled=True)  254 us
    psum x1, waiting for transfers between devices, body(): lax.psum((jnp.sum(master_gate * master_gate, axis=1), jnp.sum(master_up *...  71.4 us
    reduce_sum x1, other arithmetic, body(): jnp.sum(master_up * master_up, axis=1)  17.3 us
  transfers between devices with their start and end apart: 3, of which 2 were waited for; matrix products, arithmetic and copies ran while one was open for 4% of the time, Pallas kernels for 0%

commit v1 on v0

v1 whole, which is shorter than its diff:
```python
import functools

import jax
import jax.numpy as jnp
from jax import lax
from jax.experimental import pallas as pl
from jax.experimental.pallas import tpu as pltpu
from jax.sharding import PartitionSpec as P

MESH = pl.DeviceIdType.MESH
RING = 3


def kernel(
    groups, members, local, rows,
    gate, up, part_router,
    final_gate, final_up, scale_gate, scale_up, router,
    held, narrow, partial, arrived, scales,
    load_sem, send_sem, recv_sem, own_sem,
    sum_send, sum_recv, scale_send, scale_recv,
    row_send, row_recv, col_send, col_recv, router_sem,
):
    group, me = lax.axis_index("ep"), lax.axis_index("fsdp")
    steps = 2 * local

    def peer(j):
        return lax.rem(me + j, members)

    def group_peer(j):
        return lax.rem(group + j, groups)

    def source(step):
        return (gate, up)[step // local], (final_gate, final_up)[step // local], step % local

    order = [*range(1, steps), *range(1, steps)]

    def load(step, slot, j):
        master, _, index = source(step)
        return pltpu.make_async_copy(
            master.at[peer(j) * local + index], held.at[slot, j], load_sem.at[slot, j]
        )

    def start_load(step, slot):
        @pl.loop(0, members)
        def _(j):
            load(step, slot, j).start()

    def start_place(place):
        if place < len(order):
            start_load(order[place], 1 + place % RING)

    def sum_copy(step, j):
        return pltpu.make_async_remote_copy(
            src_ref=partial.at[step, j], dst_ref=arrived.at[step, j],
            send_sem=sum_send.at[step, j], recv_sem=sum_recv.at[step, j],
            device_id=(group, peer(j)), device_id_type=MESH,
        )

    def scale_copy(step, j):
        return pltpu.make_async_remote_copy(
            src_ref=scales.at[step, 0], dst_ref=scales.at[step, j],
            send_sem=scale_send.at[step, j], recv_sem=scale_recv.at[step, j],
            device_id=(group, peer(j)), device_id_type=MESH,
        )

    def my_rows(final, index):
        return final.at[index, pl.ds(pl.multiple_of(me * rows, rows), rows), :]

    def data_copy(step, j):
        _, final, index = source(step)
        return pltpu.make_async_remote_copy(
            src_ref=narrow.at[step % RING, j], dst_ref=my_rows(final, index),
            send_sem=send_sem.at[step, j], recv_sem=recv_sem.at[step, j],
            device_id=(group, peer(j)), device_id_type=MESH,
        )

    def own_copy(step):
        _, final, index = source(step)
        return pltpu.make_async_copy(narrow.at[step % RING, 0], my_rows(final, index), own_sem.at[step])

    width, depth = part_router.shape
    my_group_rows = pl.ds(pl.multiple_of(group * width, width), width)
    my_block = router.at[my_group_rows, pl.ds(pl.multiple_of(me * depth, depth), depth)]

    def row_copy(j):
        return pltpu.make_async_remote_copy(
            src_ref=part_router, dst_ref=my_block, send_sem=row_send.at[j], recv_sem=row_recv.at[j],
            device_id=(group, peer(j)), device_id_type=MESH,
        )

    def col_copy(j):
        return pltpu.make_async_remote_copy(
            src_ref=router.at[my_group_rows, :], dst_ref=router.at[my_group_rows, :],
            send_sem=col_send.at[j], recv_sem=col_recv.at[j],
            device_id=(group_peer(j), me), device_id_type=MESH,
        )

    start_load(0, 0)
    for place in range(RING):
        start_place(place)

    barrier = pltpu.get_barrier_semaphore()
    for j in range(1, members):
        pl.semaphore_signal(barrier, inc=1, device_id=(group, peer(j)), device_id_type=MESH)
    for j in range(1, groups):
        pl.semaphore_signal(barrier, inc=1, device_id=(group_peer(j), me), device_id_type=MESH)
    pl.semaphore_wait(barrier, members + groups - 2)

    def sums(step, slot):
        @pl.loop(0, members)
        def _(j):
            load(step, slot, j).wait()
            block = held[slot, j]
            partial[step, j] = jnp.sum(block * block, axis=0, keepdims=True)

        @pl.loop(1, members)
        def _(j):
            sum_copy(step, j).start()

    def total(step):
        @pl.loop(1, members)
        def _(j):
            sum_copy(step, j).wait_recv()

        value = partial[step, 0]
        for j in range(1, members):
            value = value + arrived[step, j]
        value = jnp.sqrt(value)
        scales[step, 0] = value
        index = step % local
        (scale_gate, scale_up)[step // local][index : index + 1, :] = value

        @pl.loop(1, members)
        def _(j):
            scale_copy(step, j).start()

    def scale_and_send(step, slot, reload):
        @pl.loop(1, members)
        def _(j):
            scale_copy(step, j).wait_recv()

        if step >= RING:
            own_copy(step - RING).wait()

            @pl.loop(1, members)
            def _(j):
                data_copy(step - RING, j).wait_send()

        @pl.loop(0, members)
        def _(j):
            if reload:
                load(step, slot, j).wait()
            inverse = 1.0 / scales[step, lax.rem(members - j, members)]
            narrow[step % RING, j] = (held[slot, j] * inverse).astype(jnp.bfloat16)

        @pl.loop(1, members)
        def _(j):
            data_copy(step, j).start()

        own_copy(step).start()

    sums(0, 0)
    ready = 0
    for step in range(1, steps):
        place = step - 1
        sums(step, 1 + place % RING)
        start_place(place + RING)
        if step >= RING:
            total(ready)
            ready += 1
    if ready == 0:
        total(0)
        ready = 1
    scale_and_send(0, 0, False)
    for step in range(ready, steps):
        total(step)

    router_own = pltpu.make_async_copy(part_router, my_block, router_sem.at[0])
    router_own.start()
    for j in range(1, members):
        row_copy(j).start()

    for step in range(1, steps):
        place = steps - 2 + step
        scale_and_send(step, 1 + place % RING, True)
        start_place(place + RING)

    router_own.wait()
    for j in range(1, members):
        row_copy(j).wait()
    for j in range(1, groups):
        col_copy(j).start()

    for step in range(steps):
        @pl.loop(1, members)
        def _(j):
            sum_copy(step, j).wait_send()
            scale_copy(step, j).wait_send()
            data_copy(step, j).wait_recv()

        if step >= steps - RING:
            own_copy(step).wait()

            @pl.loop(1, members)
            def _(j):
                data_copy(step, j).wait_send()

    for j in range(1, groups):
        col_copy(j).wait()


def exchange(groups, members, master_gate, master_up, part_router):
    experts, rows, inner = master_gate.shape
    local = experts // members
    steps = 2 * local
    width, depth = part_router.shape
    anywhere = pl.BlockSpec(memory_space=pl.ANY)
    in_vmem = pl.BlockSpec(memory_space=pltpu.VMEM)
    final = jax.ShapeDtypeStruct((local, members * rows, inner), jnp.bfloat16)
    scale = jax.ShapeDtypeStruct((local, inner), jnp.float32)
    dma = pltpu.SemaphoreType.DMA
    return pl.pallas_call(
        functools.partial(kernel, groups, members, local, rows),
        out_shape=(
            final, final, scale, scale,
            jax.ShapeDtypeStruct((groups * width, members * depth), jnp.bfloat16),
        ),
        in_specs=[anywhere] * 3,
        out_specs=(anywhere, anywhere, in_vmem, in_vmem, anywhere),
        scratch_shapes=[
            pltpu.VMEM((1 + RING, members, rows, inner), jnp.float32),
            pltpu.VMEM((RING, members, rows, inner), jnp.bfloat16),
            pltpu.VMEM((steps, members, 1, inner), jnp.float32),
            pltpu.VMEM((steps, members, 1, inner), jnp.float32),
            pltpu.VMEM((steps, members, 1, inner), jnp.float32),
            dma((1 + RING, members)),
            dma((steps, members)), dma((steps, members)), dma((steps,)),
            dma((steps, members)), dma((steps, members)),
            dma((steps, members)), dma((steps, members)),
            dma((members,)), dma((members,)), dma((groups,)), dma((groups,)), dma((1,)),
        ],
        compiler_params=pltpu.CompilerParams(
            collective_id=0, has_side_effects=True, vmem_limit_bytes=56 * 1024 * 1024
        ),
    )(master_gate, master_up, part_router)


def solution(mesh):
    groups, members = mesh.shape["ep"], mesh.shape["fsdp"]

    def body(master_gate, master_up, router_weight, router_gain):
        part_router = (router_weight * router_gain[:, None]).astype(jnp.bfloat16).T
        final_gate, final_up, scale_gate, scale_up, router = exchange(
            groups, members, master_gate, master_up, part_router
        )
        return (final_gate, final_up, scale_gate, scale_up, router.T)

    return jax.shard_map(
        body,
        mesh=mesh,
        in_specs=(P("ep", "fsdp", None), P("ep", "fsdp", None), P("fsdp", "ep"), P("fsdp")),
        out_specs=(
            P(("ep", "fsdp"), None, None),
            P(("ep", "fsdp"), None, None),
            P(("ep", "fsdp"), None),
            P(("ep", "fsdp"), None),
            P(),
        ),
        check_vma=False,
    )
```

time: 724 us -> 591 us (0.82)
  Pallas kernels: 0 us -> 568 us
  waiting for transfers between devices: 325 us -> 0 us
  blocking collectives: 296 us -> 0 us
  other arithmetic: 44.7 us -> 1.37 us
  starting transfers between devices: 15.3 us -> 0 us
  between operations: 14.1 us -> 0.65 us
    pallas_call x0 -> x1, Pallas kernels: none -> 568 us  [exchange(): pl.pallas_call(functools.partial(kernel, groups, members, local, rows), o...]
    all_gather x2 -> x0, blocking collectives: 296 us -> none  [the longest x1 288 us: body(): row_router = lax.all_gather(part_router, 'fsdp', axis=0, tiled=True)]
    all_to_all x2 -> x0, waiting for transfers between devices: 254 us -> none  [the longest x1 254 us: body(): lax.all_to_all(narrow_gate, 'fsdp', split_axis=0, concat_axis=1, tiled=True)]
    psum x1 -> x0, waiting for transfers between devices: 71.4 us -> none  [body(): lax.psum((jnp.sum(master_gate * master_gate, axis=1), jnp.sum(master_up *...]
    convert_element_type x3 -> x0, other arithmetic: 27.5 us -> none  [the longest x1 13.8 us: body(): (master_up / jnp.expand_dims(scale_up, 1)).astype(jnp.bfloat16)]
    all_to_all x2 -> x0, local copies, waits for them, and re-layouts: 21.4 us -> none  [the longest x1 10.7 us: body(): lax.all_to_all(narrow_up, 'fsdp', split_axis=0, concat_axis=1, tiled=True)]
    unnamed x7 -> x11, local copies, waits for them, and re-layouts: 1.02 us -> 21 us
    reduce_sum x1 -> x0, other arithmetic: 17.3 us -> none  [body(): jnp.sum(master_up * master_up, axis=1)]
  transfers between devices with their start and end apart: 3 -> 0, of which waited for: 2 -> 0; matrix products, arithmetic and copies ran while one was open for 4% -> 0% of each run, Pallas kernels for 0% -> 0%
where the time goes in v1:
time: 591 us
  Pallas kernels  568 us (96%)
  local copies, waits for them, and re-layouts  21 us (4%)
    pallas_call x1, Pallas kernels, exchange(): pl.pallas_call(functools.partial(kernel, groups, members, local, rows), o...  568 us
    unnamed x11, local copies, waits for them, and re-layouts  21 us

profile of v1, /device:TPU:12, one launch (start us, length us, event | category | flops | bytes accessed | tf_op | source)
XLA Modules:
  0.0 591.2 jit_solution(10749150166286478489)
XLA Ops:
  0.6 1.4 fusion.part_router
  2.0 568.2 %shard_map.83 = (bf16[4,2048,768]{2,1,0:T(8,128)(2,1)}, bf16[4,2048,768]{2,1,0:T(8,128)(2,1)}, f32[4,768]{1,0:T(4,128)}, f32[4,768]{1,0:T(4,128)}, bf16[128,2048]{1,0:T(8,128)(2,1)}) custom-call(f32[32,256,768]{2,1,0:T(8,128)} %gate.1, f32[32,256,768]{2,1,0:T(8,128)} %up.1, bf16[32,256]{1,0:T(8,128)(2,1)} %fusion.part_router), custom_call_target="tpu_custom_call" | custom-call | tf_op jit(solution)/shard_map/pallas_call | solution.py:222
  570.2 2.0 copy.9
  572.2 0.0 copy-start
  572.2 11.0 %copy.14 = bf16[4,2048,768]{2,1,0:T(8,128)(2,1)} copy(bf16[4,2048,768]{2,1,0:T(8,128)(2,1)} %get-tuple-element.25) | data formatting | bytes 25165824
  583.2 2.0 copy-done
  585.2 0.0 copy-start.2
  585.2 0.0 copy-start.1
  585.2 4.8 copy.15
  590.0 0.0 copy-done.2
  590.0 0.6 copy.16
  590.6 0.0 copy-done.1
  590.6 0.6 copy.17
Async XLA Ops:
  572.2 13.0 %copy-start = (bf16[4,2048,768]{2,1,0:T(8,128)(2,1)S(1)}, bf16[4,2048,768]{2,1,0:T(8,128)(2,1)}, u32[]{:S(2)}) copy-start(bf16[4,2048,768]{2,1,0:T(8,128)(2,1)} %get-tuple-element.26) | copy-start | bytes 37748740
  585.2 4.8 copy-start.2
  585.2 5.4 copy-start.1

commit v2 on v1

--- a/solution.py
+++ b/solution.py
@@ -8,7 +8,8 @@
 from jax.sharding import PartitionSpec as P
 
 MESH = pl.DeviceIdType.MESH
-RING = 3
+RING = 2
+SLOTS = 3
 
 
 def kernel(
@@ -16,7 +17,7 @@
     gate, up, part_router,
     final_gate, final_up, scale_gate, scale_up, router,
     held, narrow, partial, arrived, scales,
-    load_sem, send_sem, recv_sem, own_sem,
+    load_sem, send_sem, recv_sem,
     sum_send, sum_recv, scale_send, scale_recv,
     row_send, row_recv, col_send, col_recv, router_sem,
 ):
@@ -69,14 +70,10 @@
     def data_copy(step, j):
         _, final, index = source(step)
         return pltpu.make_async_remote_copy(
-            src_ref=narrow.at[step % RING, j], dst_ref=my_rows(final, index),
+            src_ref=narrow.at[step % SLOTS, j], dst_ref=my_rows(final, index),
             send_sem=send_sem.at[step, j], recv_sem=recv_sem.at[step, j],
             device_id=(group, peer(j)), device_id_type=MESH,
         )
-
-    def own_copy(step):
-        _, final, index = source(step)
-        return pltpu.make_async_copy(narrow.at[step % RING, 0], my_rows(final, index), own_sem.at[step])
 
     width, depth = part_router.shape
     my_group_rows = pl.ds(pl.multiple_of(group * width, width), width)
@@ -85,7 +82,23 @@
     def row_copy(j):
         return pltpu.make_async_remote_copy(
             src_ref=part_router, dst_ref=my_block, send_sem=row_send.at[j], recv_sem=row_recv.at[j],
-            device_id=(group, peer(j)), device_id_type=MESH,
+            device_id=(group, near_peer(j)), device_id_type=MESH,
+        )
+
+    half = members // 2
+    near = [*range(1, half), half]
+
+    def near_peer(j):
+        if j == half:
+            return peer(half)
+        return me // half * half + lax.rem(me % half + j, half)
+
+    def relay_copy(j):
+        other = pl.ds(pl.multiple_of(peer(half) * depth, depth), depth)
+        block = router.at[my_group_rows, other]
+        return pltpu.make_async_remote_copy(
+            src_ref=block, dst_ref=block, send_sem=row_send.at[half + j], recv_sem=row_recv.at[half + j],
+            device_id=(group, near_peer(j)), device_id_type=MESH,
         )
 
     def col_copy(j):
@@ -139,55 +152,62 @@
         def _(j):
             scale_copy(step, j).wait_recv()
 
-        if step >= RING:
-            own_copy(step - RING).wait()
-
+        if step >= SLOTS:
             @pl.loop(1, members)
             def _(j):
-                data_copy(step - RING, j).wait_send()
-
-        @pl.loop(0, members)
+                data_copy(step - SLOTS, j).wait_send()
+
+        @pl.loop(1, members)
         def _(j):
             if reload:
                 load(step, slot, j).wait()
             inverse = 1.0 / scales[step, lax.rem(members - j, members)]
-            narrow[step % RING, j] = (held[slot, j] * inverse).astype(jnp.bfloat16)
+            narrow[step % SLOTS, j] = (held[slot, j] * inverse).astype(jnp.bfloat16)
 
         @pl.loop(1, members)
         def _(j):
             data_copy(step, j).start()
 
-        own_copy(step).start()
+        if reload:
+            load(step, slot, 0).wait()
+        _, final, index = source(step)
+        own = held[slot, 0] * (1.0 / scales[step, 0])
+        final[index, pl.ds(pl.multiple_of(me * rows, rows), rows), :] = own.astype(jnp.bfloat16)
 
     sums(0, 0)
-    ready = 0
-    for step in range(1, steps):
-        place = step - 1
-        sums(step, 1 + place % RING)
-        start_place(place + RING)
-        if step >= RING:
-            total(ready)
-            ready += 1
-    if ready == 0:
-        total(0)
-        ready = 1
+    lead = min(SLOTS, steps)
+    for step in range(1, lead):
+        sums(step, 1 + (step - 1) % RING)
+        start_place(step - 1 + RING)
+    total(0)
     scale_and_send(0, 0, False)
-    for step in range(ready, steps):
+    for step in range(lead, steps):
+        sums(step, 1 + (step - 1) % RING)
+        start_place(step - 1 + RING)
+    for step in range(1, lead):
         total(step)
 
     router_own = pltpu.make_async_copy(part_router, my_block, router_sem.at[0])
     router_own.start()
-    for j in range(1, members):
+    for j in near:
         row_copy(j).start()
 
     for step in range(1, steps):
+        if step == 2:
+            for late in range(lead, steps):
+                total(late)
         place = steps - 2 + step
         scale_and_send(step, 1 + place % RING, True)
         start_place(place + RING)
+        if step == steps // 2:
+            for j in near:
+                row_copy(j).wait()
+            for j in range(1, members // 2):
+                relay_copy(j).start()
 
     router_own.wait()
-    for j in range(1, members):
-        row_copy(j).wait()
+    for j in range(1, members // 2):
+        relay_copy(j).wait()
     for j in range(1, groups):
         col_copy(j).start()
 
@@ -198,9 +218,7 @@
             scale_copy(step, j).wait_send()
             data_copy(step, j).wait_recv()
 
-        if step >= steps - RING:
-            own_copy(step).wait()
-
+        if step >= steps - SLOTS:
             @pl.loop(1, members)
             def _(j):
                 data_copy(step, j).wait_send()
@@ -216,7 +234,7 @@
     width, depth = part_router.shape
     anywhere = pl.BlockSpec(memory_space=pl.ANY)
     in_vmem = pl.BlockSpec(memory_space=pltpu.VMEM)
-    final = jax.ShapeDtypeStruct((local, members * rows, inner), jnp.bfloat16)
+    final = pltpu.VMEM((local, members * rows, inner), jnp.bfloat16)
     scale = jax.ShapeDtypeStruct((local, inner), jnp.float32)
     dma = pltpu.SemaphoreType.DMA
     return pl.pallas_call(
@@ -226,23 +244,47 @@
             jax.ShapeDtypeStruct((groups * width, members * depth), jnp.bfloat16),
         ),
         in_specs=[anywhere] * 3,
-        out_specs=(anywhere, anywhere, in_vmem, in_vmem, anywhere),
+        out_specs=(in_vmem, in_vmem, in_vmem, in_vmem, anywhere),
         scratch_shapes=[
             pltpu.VMEM((1 + RING, members, rows, inner), jnp.float32),
-            pltpu.VMEM((RING, members, rows, inner), jnp.bfloat16),
+            pltpu.VMEM((SLOTS, members, rows, inner), jnp.bfloat16),
             pltpu.VMEM((steps, members, 1, inner), jnp.float32),
             pltpu.VMEM((steps, members, 1, inner), jnp.float32),
             pltpu.VMEM((steps, members, 1, inner), jnp.float32),
             dma((1 + RING, members)),
-            dma((steps, members)), dma((steps, members)), dma((steps,)),
+            dma((steps, members)), dma((steps, members)),
             dma((steps, members)), dma((steps, members)),
             dma((steps, members)), dma((steps, members)),
             dma((members,)), dma((members,)), dma((groups,)), dma((groups,)), dma((1,)),
         ],
         compiler_params=pltpu.CompilerParams(
-            collective_id=0, has_side_effects=True, vmem_limit_bytes=56 * 1024 * 1024
+            collective_id=0, has_side_effects=True, vmem_limit_bytes=34 * 1024 * 1024
         ),
     )(master_gate, master_up, part_router)
+
+
+def store_kernel(gate, up, final_gate, final_up, sem):
+    copies = [
+        pltpu.make_async_copy(landed.at[index], final.at[index], sem.at[which, index])
+        for which, (landed, final) in enumerate(((gate, final_gate), (up, final_up)))
+        for index in range(landed.shape[0])
+    ]
+    for copy in copies:
+        copy.start()
+    for copy in copies:
+        copy.wait()
+
+
+def store(gate, up):
+    final = jax.ShapeDtypeStruct(gate.shape, gate.dtype)
+    return pl.pallas_call(
+        store_kernel,
+        out_shape=(final, final),
+        in_specs=[pl.BlockSpec(memory_space=pltpu.VMEM)] * 2,
+        out_specs=(pl.BlockSpec(memory_space=pl.ANY),) * 2,
+        scratch_shapes=[pltpu.SemaphoreType.DMA((2, gate.shape[0]))],
+        compiler_params=pltpu.CompilerParams(vmem_limit_bytes=2 * 1024 * 1024),
+    )(gate, up)
 
 
 def solution(mesh):
@@ -253,6 +295,7 @@
         final_gate, final_up, scale_gate, scale_up, router = exchange(
             groups, members, master_gate, master_up, part_router
         )
+        final_gate, final_up = store(final_gate, final_up)
         return (final_gate, final_up, scale_gate, scale_up, router.T)
 
     return jax.shard_map(

time: 591 us -> 577 us (0.976)
  local copies, waits for them, and re-layouts: 21 us -> 2.21 us
    unnamed x11 -> x9, local copies, waits for them, and re-layouts: 21 us -> 2.21 us
    pallas_call x0 -> x1, Pallas kernels: none -> 8.54 us  [store(): pl.pallas_call(store_kernel, out_shape=(final, final), in_specs=[pl.Block...]
where the time goes in v2:
time: 577 us
  Pallas kernels  572 us (99%)
    pallas_call x1, Pallas kernels, exchange(): pl.pallas_call(functools.partial(kernel, groups, members, local, rows), o...  564 us

profile of v2, /device:TPU:12, one launch (start us, length us, event | category | flops | bytes accessed | tf_op | source)
XLA Modules:
  0.0 576.6 jit_solution(4308434766433284731)
XLA Ops:
  0.6 1.4 fusion.part_router
  2.0 563.8 %shard_map.83 = (bf16[4,2048,768]{2,1,0:T(8,128)(2,1)S(1)}, bf16[4,2048,768]{2,1,0:T(8,128)(2,1)S(1)}, f32[4,768]{1,0:T(4,128)}, f32[4,768]{1,0:T(4,128)}, bf16[128,2048]{1,0:T(8,128)(2,1)}) custom-call(f32[32,256,768]{2,1,0:T(8,128)} %gate.1, f32[32,256,768]{2,1,0:T(8,128)} %up.1, bf16[32,256]{1,0:T(8,128)(2,1)} %fusion.part_router), custom_call_target="tpu_custom_call" | custom-call | tf_op jit(solution)/shard_map/pallas_call | solution.py:240
  565.8 0.0 copy-start
  565.8 0.0 copy-start.2
  565.8 0.0 copy-start.1
  565.8 8.5 %shard_map.84 = (bf16[4,2048,768]{2,1,0:T(8,128)(2,1)}, bf16[4,2048,768]{2,1,0:T(8,128)(2,1)}) custom-call(bf16[4,2048,768]{2,1,0:T(8,128)(2,1)S(1)} %get-tuple-element.12.gate, bf16[4,2048,768]{2,1,0:T(8,128)(2,1)S(1)} %get-tuple-element.13.up), custom_call_target="tpu_custom_call" | custom-call | tf_op jit(solution)/shard_map/pallas_call | solution.py:280
  574.4 0.0 copy-done
  574.4 1.0 copy.9
  575.4 0.0 copy-done.2
  575.4 0.6 copy.12
  576.0 0.0 copy-done.1
  576.0 0.6 copy.13
Async XLA Ops:
  565.8 8.6 %copy-start = (bf16[128,2048]{1,0:T(8,128)(2,1)S(1)}, bf16[128,2048]{1,0:T(8,128)(2,1)}, u32[]{:S(2)}) copy-start(bf16[128,2048]{1,0:T(8,128)(2,1)} %get-tuple-element.18) | copy-start | bytes 1572868
  565.8 9.6 %copy-start.2 = (f32[4,768]{1,0:T(4,128)S(1)}, f32[4,768]{1,0:T(4,128)}, u32[]{:S(2)}) copy-start(f32[4,768]{1,0:T(4,128)} %get-tuple-element.31) | copy-start | bytes 36868
  565.8 10.2 %copy-start.1 = (f32[4,768]{1,0:T(4,128)S(1)}, f32[4,768]{1,0:T(4,128)}, u32[]{:S(2)}) copy-start(f32[4,768]{1,0:T(4,128)} %get-tuple-element.32) | copy-start | bytes 36868
